TPU v7x, 256 devices: a whole 4x4x8 slice. The times are simulated.
256 devices in a mesh: lat: 16 (over y_hi, z), lon: 16 (over x, y_lo, core).
Axes of the slice: x: 4, y: 4 (y_hi: 2, y_lo: 2; y = y_hi * 2 + y_lo), z: 8, core: 2. Of those that a mesh axis runs over, the one named last changes fastest.
Arguments:
- predicted_state: bfloat16 [222, 640, 2048], P(None, 'lat', 'lon'), may hold values from -30 to 30
- observed_state: bfloat16 [222, 640, 2048], P(None, 'lat', 'lon'), may hold values from -30 to 30
- longterm_average_state: bfloat16 [222, 640, 2048], P(None, 'lat', 'lon'), may hold values from -30 to 30
Outputs:
- blurred_mismatch_map: bfloat16 [222, 640, 2048], P(None, 'lat', 'lon')
- quadratic_mean_mistake: float32 [222], replicated
- pattern_agreement: float32 [222], replicated
All inputs are finite; a program needn't handle non-finite values.
Results may differ from a plain program's by a relative error of at most 0.00155.
Values may be sent and summed in bfloat16 or wider, within the bound.
A program may use at most 128 MiB of HBM per device.

v0:
```python
import jax
import jax.numpy as jnp
from jax import lax
from jax.sharding import PartitionSpec as P

epsilon = 1e-06


def extended(cells, sides, width, closed):
    for axis, dim in sides:
        count = lax.axis_size(axis)
        ends = count if closed else count - 1
        head = lax.slice_in_dim(cells, 0, width, axis=dim)
        tail = lax.slice_in_dim(cells, cells.shape[dim] - width, cells.shape[dim], axis=dim)
        cells = jnp.concatenate(
            [
                lax.ppermute(tail, axis, [(i, (i + 1) % count) for i in range(ends)]),
                cells,
                lax.ppermute(head, axis, [((i + 1) % count, i) for i in range(ends)]),
            ],
            axis=dim,
        )
    return cells


def sent_to_all(x, axis):
    length = lax.axis_size(axis)
    return lax.all_to_all(jnp.broadcast_to(x[None], (length, *x.shape)), axis, 0, 0, tiled=True)


def over_copies(x, axis):
    return sent_to_all(x, axis).sum(axis=0)


def deviation_from_normal(predicted_state, observed_state, longterm_average_state):
    normal_reference_state = longterm_average_state.astype(jnp.float32)
    return (
        predicted_state.astype(jnp.float32) - normal_reference_state,
        observed_state.astype(jnp.float32) - normal_reference_state,
    )


def vertical_sum(member):
    return member[:, :-2] + member[:, 1:-1] + member[:, 2:]


def horizontal_sum(member):
    return member[:, :, :-2] + member[:, :, 1:-1] + member[:, :, 2:]


def finish(running_accumulations, grid_cells):
    mean_fcst = running_accumulations[1] / grid_cells
    mean_true = running_accumulations[2] / grid_cells
    variance_fcst = running_accumulations[3] / grid_cells - mean_fcst * mean_fcst
    variance_true = running_accumulations[4] / grid_cells - mean_true * mean_true
    covariance = running_accumulations[5] / grid_cells - mean_fcst * mean_true
    quadratic_mean_mistake = jnp.sqrt(running_accumulations[0] / grid_cells)
    pattern_agreement = covariance / jnp.sqrt((variance_fcst + epsilon) * (variance_true + epsilon))
    return (quadratic_mean_mistake, pattern_agreement)


def local(predicted_state, observed_state, longterm_average_state):
    nearby_parallel_accumulated = predicted_state.shape[1]
    parallel_overall_accumulated = nearby_parallel_accumulated * lax.axis_size("lat")
    meridian_accumulated = predicted_state.shape[2] * lax.axis_size("lon")
    row_start = lax.axis_index("lat") * nearby_parallel_accumulated
    row_index = row_start + jnp.arange(nearby_parallel_accumulated, dtype=jnp.int32)
    stacked_inputs = jnp.stack([predicted_state, observed_state, longterm_average_state])
    rimmed = extended(stacked_inputs, (("lat", 2),), 1, False)
    stretched = deviation_from_normal(rimmed[0], rimmed[1], rimmed[2])
    vertical = jnp.stack([vertical_sum(stretched[0]), vertical_sum(stretched[1])])
    widened = extended(vertical, (("lon", 3),), 1, True)
    summed = (horizontal_sum(widened[0]), horizontal_sum(widened[1]))
    row_count = (
        3.0
        - (row_index == 0).astype(jnp.float32)
        - (row_index == parallel_overall_accumulated - 1).astype(jnp.float32)
    )
    divisor = (3.0 * row_count)[:, None]
    averaged_prediction = summed[0] / divisor
    averaged_observation = summed[1] / divisor
    prediction_mismatch = averaged_prediction - averaged_observation
    all_rows = jnp.arange(parallel_overall_accumulated, dtype=jnp.float32)
    cosine = jnp.cos(jnp.pi * (0.5 - all_rows / (parallel_overall_accumulated - 1)))
    weight_all = cosine / jnp.mean(cosine)
    cosine_factor_vector = lax.dynamic_slice_in_dim(
        weight_all, row_start, nearby_parallel_accumulated
    )[:, None]
    weighted_fcst = cosine_factor_vector * averaged_prediction
    weighted_true = cosine_factor_vector * averaged_observation
    running_accumulations = jnp.stack(
        [
            jnp.sum(cosine_factor_vector * prediction_mismatch * prediction_mismatch, axis=(1, 2)),
            jnp.sum(weighted_fcst, axis=(1, 2)),
            jnp.sum(weighted_true, axis=(1, 2)),
            jnp.sum(weighted_fcst * averaged_prediction, axis=(1, 2)),
            jnp.sum(weighted_true * averaged_observation, axis=(1, 2)),
            jnp.sum(weighted_fcst * averaged_observation, axis=(1, 2)),
        ]
    )
    totals = over_copies(over_copies(running_accumulations, "lat"), "lon")
    quadratic_mean_mistake, pattern_agreement = finish(
        totals, float(parallel_overall_accumulated * meridian_accumulated)
    )
    return (prediction_mismatch.astype(jnp.bfloat16), quadratic_mean_mistake, pattern_agreement)


def solution(mesh):
    placed = (P(None, "lat", "lon"), P(None, "lat", "lon"), P(None, "lat", "lon"))
    return jax.shard_map(
        local,
        mesh=mesh,
        in_specs=placed,
        out_specs=(P(None, "lat", "lon"), P(), P()),
        check_vma=False,
    )
```

profile of v0, /device:TPU:1, one launch (start us, length us, event | category | flops | bytes accessed | tf_op | source)
XLA Modules:
  0.0 116.5 jit_solution(1152747819263213656)
XLA Ops:
  0.6 4.5 %copy.14 = bf16[222,40,128]{0,1,2:T(8,128)(2,1)S(1)} copy(bf16[222,40,128]{2,1,0:T(8,128)(2,1)} %param.3) | data formatting | bytes 4546560 | tf_op args[0]
  5.1 5.2 %copy.15 = bf16[222,40,128]{0,1,2:T(8,128)(2,1)} copy(bf16[222,40,128]{2,1,0:T(8,128)(2,1)} %param.4) | data formatting | bytes 4546560 | tf_op args[1]
  10.3 5.3 %copy.16 = bf16[222,40,128]{0,1,2:T(8,128)(2,1)} copy(bf16[222,40,128]{2,1,0:T(8,128)(2,1)} %param.5) | data formatting | bytes 4546560 | tf_op args[2]
  15.6 2.3 %pad_maximum_fusion.4 = (bf16[3,222,1,128]{1,2,3,0:T(2,128)(2,1)S(1)}, bf16[3,222,1,128]{1,2,3,0:T(2,128)(2,1)S(1)}) fusion(bf16[1,222,40,128]{1,2,3,0:T(8,128)(2,1)} %bitcast.27, bf16[1,222,40,128]{1,2,3,0:T(8,128)(2,1)} %bitcast.25, bf16[1,222,40,128]{1,2,3,0:T(8,128)(2,1)S(1)} %bitcast.23), kind=kLoop, calls=%fused_computation.33 | loop fusion | flops 1022976 | bytes 7160832 | tf_op jit(solution)/shard_map/slice | solution.py:14
  17.8 5.1 %collective-permute-start = (bf16[3,222,1,128]{1,2,3,0:T(2,128)(2,1)S(1)}, bf16[3,222,1,128]{1,2,3,0:T(2,128)(2,1)}, u32[]{:S(2)}, u32[]{:S(2)}) collective-permute-start(bf16[3,222,1,128]{1,2,3,0:T(2,128)(2,1)S(1)} %get-tuple-element.26), channel_id=1, source_target_pairs={{0,16},{16,32},{32,48},{48,64},{64,80},{80,96},{96,112},{112,128},... | collective-permute-start | bytes 511496 | tf_op jit(solution)/shard_map/ppermute | solution.py:17
  23.0 1.3 %collective-permute-start.1 = (bf16[3,222,1,128]{1,2,3,0:T(2,128)(2,1)S(1)}, bf16[3,222,1,128]{1,2,3,0:T(2,128)(2,1)}, u32[]{:S(2)}, u32[]{:S(2)}) collective-permute-start(bf16[3,222,1,128]{1,2,3,0:T(2,128)(2,1)S(1)} %get-tuple-element.27), channel_id=1, source_target_pairs={{16,0},{32,16},{48,32},{64,48},{80,64},{96,80},{112,96},{128,112},... | collective-permute-start | bytes 511496 | tf_op jit(solution)/shard_map/ppermute | solution.py:19
  24.3 0.7 fusion.11
  25.6 0.1 dynamic_slice.3
  25.7 4.3 %collective-permute-done = bf16[3,222,1,128]{1,2,3,0:T(2,128)(2,1)} collective-permute-done((bf16[3,222,1,128]{1,2,3,0:T(2,128)(2,1)S(1)}, bf16[3,222,1,128]{1,2,3,0:T(2,128)(2,1)}, u32[]{:S(2)}, u32[]{:S(2)}) %collective-permute-start) | collective-permute-done | bytes 170528 | tf_op jit(solution)/shard_map/ppermute | solution.py:17
  30.0 4.7 %collective-permute-done.1 = bf16[3,222,1,128]{1,2,3,0:T(2,128)(2,1)} collective-permute-done((bf16[3,222,1,128]{1,2,3,0:T(2,128)(2,1)S(1)}, bf16[3,222,1,128]{1,2,3,0:T(2,128)(2,1)}, u32[]{:S(2)}, u32[]{:S(2)}) %collective-permute-start.1) | collective-permute-done | bytes 170528 | tf_op jit(solution)/shard_map/ppermute | solution.py:19
  34.7 8.1 %pad_maximum_fusion.1 = bf16[3,222,42,128]{1,2,3,0:T(8,128)(2,1)S(1)} fusion(bf16[3,222,1,128]{1,2,3,0:T(2,128)(2,1)} %collective-permute-done.1, bf16[1,222,40,128]{1,2,3,0:T(8,128)(2,1)} %bitcast.28, bf16[1,222,40,128]{1,2,3,0:T(8,128)(2,1)} %bitcast.26, bf16[1,222,40,128]{1,2,3,0:T(8,128)(2,1)S(1)} %bitcast.24, ...), kind=kLoop, calls=%fused_computation.1 | loop fusion | flops 35804160 | bytes 14321664 | tf_op jit(solution)/shard_map/concatenate | solution.py:15
  42.8 3.3 %fusion = (f32[222,42,128]{0,1,2:T(8,128)S(1)}, f32[222,42,128]{0,1,2:T(8,128)}) fusion(bf16[3,222,42,128]{1,2,3,0:T(8,128)(2,1)S(1)} %pad_maximum_fusion.1), kind=kLoop, calls=%fused_computation.10 | loop fusion | flops 5967360 | bytes 16708608 | tf_op jit(solution)/shard_map/sub | solution.py:38
  46.1 11.5 %fusion.8 = (f32[1,222,40,128]{1,2,3,0:T(8,128)}, f32[1,222,40,128]{1,2,3,0:T(8,128)}) fusion(f32[222,42,128]{0,1,2:T(8,128)} %get-tuple-element.25, f32[222,42,128]{0,1,2:T(8,128)S(1)} %get-tuple-element.24), kind=kLoop, calls=%fused_computation.25 | loop fusion | flops 4546560 | bytes 36372480 | tf_op jit(solution)/shard_map/stack | solution.py:71
  57.6 0.0 copy-start
  57.6 0.0 copy-start.1
  57.6 1.0 pad_maximum_fusion.6
  58.6 3.1 %collective-permute-start.2 = (f32[2,222,40,1]{1,2,3,0:T(8,128)S(1)}, f32[2,222,40,1]{1,2,3,0:T(8,128)S(1)}, u32[]{:S(2)}, u32[]{:S(2)}) collective-permute-start(f32[2,222,40,1]{1,2,3,0:T(8,128)S(1)} %get-tuple-element.22), channel_id=1, source_target_pairs={{0,1},{1,2},{2,3},{3,4},{4,5},{5,6},{6,7},{7,8},{8,9},{9,10},{10,1... | collective-permute-start | bytes 213128 | tf_op jit(solution)/shard_map/ppermute | solution.py:17
  61.6 0.0 collective-permute-start.3
  61.7 1.5 %collective-permute-done.2 = f32[2,222,40,1]{1,2,3,0:T(8,128)S(1)} collective-permute-done((f32[2,222,40,1]{1,2,3,0:T(8,128)S(1)}, f32[2,222,40,1]{1,2,3,0:T(8,128)S(1)}, u32[]{:S(2)}, u32[]{:S(2)}) %collective-permute-start.2) | collective-permute-done | bytes 71072 | tf_op jit(solution)/shard_map/ppermute | solution.py:17
  63.1 3.3 %collective-permute-done.3 = f32[2,222,40,1]{1,2,3,0:T(8,128)S(1)} collective-permute-done((f32[2,222,40,1]{1,2,3,0:T(8,128)S(1)}, f32[2,222,40,1]{1,2,3,0:T(8,128)S(1)}, u32[]{:S(2)}, u32[]{:S(2)}) %collective-permute-start.3) | collective-permute-done | bytes 71072 | tf_op jit(solution)/shard_map/ppermute | solution.py:19
  66.4 0.0 copy-done
  66.4 0.0 copy-done.1
  66.4 4.5 %pad_maximum_fusion = f32[2,222,40,130]{1,2,3,0:T(8,128)} fusion(f32[2,222,40,1]{1,2,3,0:T(8,128)S(1)} %collective-permute-done.3, f32[1,222,40,128]{1,2,3,0:T(8,128)S(1)} %copy-done, f32[1,222,40,128]{1,2,3,0:T(8,128)S(1)} %copy-done.1, f32[2,222,40,1]{1,2,3,0:T(8,128)S(1)} %collective-permute-done.2), kind=kLoop, calls=%fused_computation | loop fusion | flops 6926400 | bytes 18470400 | tf_op jit(solution)/shard_map/concatenate | solution.py:15
  70.9 4.8 %slice_bitcast_fusion.1 = (f32[222,40,130]{0,1,2:T(8,128)S(1)}, f32[222,40,130]{0,1,2:T(8,128)S(1)}) fusion(f32[2,222,40,130]{1,2,3,0:T(8,128)} %pad_maximum_fusion), kind=kLoop, calls=%fused_computation.13 | loop fusion | bytes 18470400 | tf_op jit(solution)/shard_map/squeeze | solution.py:73
  75.7 6.8 %fusion.3 = (f32[222]{0:T(256)S(1)}, f32[222]{0:T(256)S(1)}, f32[222]{0:T(256)S(1)}, f32[222]{0:T(256)S(1)}, f32[222]{0:T(256)S(1)}, /*index=5*/f32[222]{0:T(256...) fusion(f32[40]{0:T(128)S(1)} %dynamic_slice.3, f32[40]{0:T(128)S(1)} %fusion.19, f32[222,40,130]{0,1,2:T(8,128)S(1)} %get-tuple-element.21, ...), kind=kLoop, calls=%fused_computation.15 | loop fusion | flops 22731468 | bytes 36378128 | tf_op jit(solution)/shard_map/reduce_sum | solution.py:98
  82.6 18.5 %all_to_all.10 = f32[16,6,222]{2,1,0:T(8,128)S(1)} all-to-all(f32[16,6,222]{2,1,0:T(8,128)S(1)} %broadcast_in_dim.4), channel_id=1, replica_groups=mesh['lat'=16,'lon'=16] {'lat'}, dimensions={0} | all-to-all | bytes 170496 | tf_op jit(solution)/shard_map/all_to_all | solution.py:28
  101.1 0.7 broadcast_in_dim.5
  101.8 5.4 %all-to-all-start.1 = ((f32[16,6,222]{2,1,0:T(8,128)}), f32[16,6,222]{2,1,0:T(8,128)S(1)}, u32[]{:S(2)}, u32[]{:S(2)}) async-start(f32[16,6,222]{2,1,0:T(8,128)} %broadcast_in_dim.5), calls=%async_computation.1 | async-start | bytes 262144 | tf_op jit(solution)/shard_map/all_to_all | solution.py:28
  107.2 4.9 %subtract_convert_fusion = bf16[222,40,128]{0,1,2:T(8,128)(2,1)S(1)} fusion(f32[222,40,128]{0,1,2:T(8,128)} %get-tuple-element.19, f32[222,40,128]{0,1,2:T(8,128)} %get-tuple-element.18), kind=kLoop, calls=%fused_computation.30 | loop fusion | flops 2273280 | bytes 11366400 | tf_op jit(solution)/shard_map/convert_element_type | solution.py:105
  112.1 3.8 %copy.19 = bf16[222,40,128]{2,1,0:T(8,128)(2,1)} copy(bf16[222,40,128]{0,1,2:T(8,128)(2,1)S(1)} %subtract_convert_fusion) | data formatting | bytes 4546560
  115.9 0.0 all-to-all-done.1
  115.9 0.6 fusion.15
  (6 shorter events, 0.1 us)
Async XLA Ops:
  17.8 12.1 %collective-permute-start = (bf16[3,222,1,128]{1,2,3,0:T(2,128)(2,1)S(1)}, bf16[3,222,1,128]{1,2,3,0:T(2,128)(2,1)}, u32[]{:S(2)}, u32[]{:S(2)}) collective-permute-start(bf16[3,222,1,128]{1,2,3,0:T(2,128)(2,1)S(1)} %get-tuple-element.26), channel_id=1, source_target_pairs={{0,16},{16,32},{32,48},{48,64},{64,80},{80,96},{96,112},{112,128},... | collective-permute-start | bytes 511496 | tf_op jit(solution)/shard_map/ppermute | solution.py:17
  23.0 11.7 %collective-permute-start.1 = (bf16[3,222,1,128]{1,2,3,0:T(2,128)(2,1)S(1)}, bf16[3,222,1,128]{1,2,3,0:T(2,128)(2,1)}, u32[]{:S(2)}, u32[]{:S(2)}) collective-permute-start(bf16[3,222,1,128]{1,2,3,0:T(2,128)(2,1)S(1)} %get-tuple-element.27), channel_id=1, source_target_pairs={{16,0},{32,16},{48,32},{64,48},{80,64},{96,80},{112,96},{128,112},... | collective-permute-start | bytes 511496 | tf_op jit(solution)/shard_map/ppermute | solution.py:19
  57.6 8.8 %copy-start = (f32[1,222,40,128]{1,2,3,0:T(8,128)S(1)}, f32[1,222,40,128]{1,2,3,0:T(8,128)}, u32[]{:S(2)}) copy-start(f32[1,222,40,128]{1,2,3,0:T(8,128)} %get-tuple-element.30) | copy-start | bytes 13639684
  57.6 8.8 %copy-start.1 = (f32[1,222,40,128]{1,2,3,0:T(8,128)S(1)}, f32[1,222,40,128]{1,2,3,0:T(8,128)}, u32[]{:S(2)}) copy-start(f32[1,222,40,128]{1,2,3,0:T(8,128)} %get-tuple-element.31) | copy-start | bytes 13639684
  58.6 4.6 %collective-permute-start.2 = (f32[2,222,40,1]{1,2,3,0:T(8,128)S(1)}, f32[2,222,40,1]{1,2,3,0:T(8,128)S(1)}, u32[]{:S(2)}, u32[]{:S(2)}) collective-permute-start(f32[2,222,40,1]{1,2,3,0:T(8,128)S(1)} %get-tuple-element.22), channel_id=1, source_target_pairs={{0,1},{1,2},{2,3},{3,4},{4,5},{5,6},{6,7},{7,8},{8,9},{9,10},{10,1... | collective-permute-start | bytes 213128 | tf_op jit(solution)/shard_map/ppermute | solution.py:17
  61.6 4.7 %collective-permute-start.3 = (f32[2,222,40,1]{1,2,3,0:T(8,128)S(1)}, f32[2,222,40,1]{1,2,3,0:T(8,128)S(1)}, u32[]{:S(2)}, u32[]{:S(2)}) collective-permute-start(f32[2,222,40,1]{1,2,3,0:T(8,128)S(1)} %get-tuple-element.23), channel_id=1, source_target_pairs={{1,0},{2,1},{3,2},{4,3},{5,4},{6,5},{7,6},{8,7},{9,8},{10,9},{11,1... | collective-permute-start | bytes 213128 | tf_op jit(solution)/shard_map/ppermute | solution.py:19
  101.8 14.1 %all-to-all-start.1 = ((f32[16,6,222]{2,1,0:T(8,128)}), f32[16,6,222]{2,1,0:T(8,128)S(1)}, u32[]{:S(2)}, u32[]{:S(2)}) async-start(f32[16,6,222]{2,1,0:T(8,128)} %broadcast_in_dim.5), calls=%async_computation.1 | async-start | bytes 262144 | tf_op jit(solution)/shard_map/all_to_all | solution.py:28
where the time goes:
time: 117 us; the launch traced here: 116 us
  other arithmetic  43.8 us (37%)
  local copies, waits for them, and re-layouts  24.3 us (21%)
  blocking collectives  18.5 us (16%)
  starting transfers between devices  14.9 us (13%)
  waiting for transfers between devices  13.7 us (12%)
  between operations  1.35 us (1%)
    unnamed x8, local copies, waits for them, and re-layouts  18.7 us
    all_to_all x1, blocking collectives, sent_to_all(): lax.all_to_all(jnp.broadcast_to(x[None], (length, *x.shape)), axis, 0, 0,...  18.5 us
    concatenate x2, other arithmetic, extended(): jnp.concatenate([lax.ppermute(tail, axis, [(i, (i + 1) % count) for i in...  12.6 us
    another operation x1, other arithmetic, local(): jnp.stack([vertical_sum(stretched[0]), vertical_sum(stretched[1])])  11.5 us
    ppermute x2, starting transfers between devices, extended(): lax.ppermute(tail, axis, [(i, (i + 1) % count) for i in range(ends)])  8.2 us
    ppermute x2, waiting for transfers between devices, extended(): lax.ppermute(head, axis, [((i + 1) % count, i) for i in range(ends)])  7.94 us
    reduce_sum x1, other arithmetic, local(): jnp.sum(weighted_fcst * averaged_observation, axis=(1, 2))  6.83 us
    ppermute x2, waiting for transfers between devices, extended(): lax.ppermute(tail, axis, [(i, (i + 1) % count) for i in range(ends)])  5.77 us
  transfers between devices with their start and end apart: 5, of which 4 were waited for; matrix products, arithmetic and copies ran while one was open for 8% of the time, Pallas kernels for 0%

commit v1 on v0

v1 whole, which is shorter than its diff:
```python
import functools
import math

import jax
import jax.numpy as jnp
import numpy as np
from jax import lax
from jax.experimental import pallas as pl
from jax.experimental.pallas import tpu as pltpu
from jax.sharding import PartitionSpec as P

epsilon = 1e-06
MESH = pl.DeviceIdType.MESH
F32 = jnp.float32
LANES = 128
CHUNKS = 8


def mean_cosine(rows):
    i = np.arange(rows, dtype=np.float64)
    return float(np.mean(np.cos(np.pi * (0.5 - i / (rows - 1)))))


def kernel(
    nlat, nlon, fields, rows, bounds,
    p_hbm, o_hbm, c_hbm,
    out_ref, rmse_ref, acc_ref,
    p, o, c, nat, slab, diff, halo, side_out, side_in, weight, sums, part, got, tot,
    in_sem, lat_send, lat_recv, lon_send, lon_recv, cor_send, cor_recv, red_send, red_recv,
):
    lat = lax.axis_index("lat")
    lon = lax.axis_index("lon")
    up = lax.rem(lat + nlat - 1, nlat)
    down = lax.rem(lat + 1, nlat)
    left = lax.rem(lon + nlon - 1, nlon)
    right = lax.rem(lon + 1, nlon)
    tiles = slab.shape[1]
    total_rows = nlat * rows

    loads = []
    for k, (lo, hi) in enumerate(bounds):
        span = pl.ds(lo * rows, (hi - lo) * rows)
        group = [
            pltpu.make_async_copy(src.at[span, :], dst.at[span, :], in_sem.at[k, n])
            for n, (src, dst) in enumerate(((p_hbm, p), (o_hbm, o), (c_hbm, c)))
        ]
        for copy in group:
            copy.start()
        loads.append(group)

    barrier = pltpu.get_barrier_semaphore()

    def greet_lon(k, carry):
        pl.semaphore_signal(
            barrier, inc=1, device_id=(lat, lax.rem(lon + k, nlon)), device_id_type=MESH
        )
        return carry

    def greet_lat(k, carry):
        pl.semaphore_signal(
            barrier, inc=1, device_id=(lax.rem(lat + k, nlat), lon), device_id_type=MESH
        )
        return carry

    corners = ((up, left), (up, right), (down, left), (down, right))
    for peer in corners:
        pl.semaphore_signal(barrier, inc=1, device_id=peer, device_id_type=MESH)
    lax.fori_loop(1, nlon, greet_lon, 0)
    lax.fori_loop(1, nlat, greet_lat, 0)

    row = (lax.broadcasted_iota(jnp.int32, (rows, 8, LANES), 0) + lat * rows).astype(F32)
    cosine = jnp.cos(jnp.pi * (0.5 - row / (total_rows - 1)))
    weight[...] = cosine * (1.0 / mean_cosine(total_rows))
    north = jnp.where(lat == 0, 1.5, 1.0).astype(F32)
    south = jnp.where(lat == nlat - 1, 1.5, 1.0).astype(F32)
    north_in = jnp.where(lat == 0, 0.0, 1.0).astype(F32)
    south_in = jnp.where(lat == nlat - 1, 0.0, 1.0).astype(F32)

    padded = tiles * LANES * rows
    if padded > fields * rows:
        for a in range(2):
            nat[a, fields * rows :, :] = jnp.zeros((padded - fields * rows, LANES), F32)
    step = 2 * rows
    for k, (lo, hi) in enumerate(bounds):
        for copy in loads[k]:
            copy.wait()

        def subtract(i, carry):
            span = pl.ds(pl.multiple_of(i * step, 16), step)
            normal = c[span, :].astype(F32)
            nat[0, span, :] = p[span, :].astype(F32) - normal
            nat[1, span, :] = o[span, :].astype(F32) - normal
            return carry

        lax.fori_loop(lo // 2, hi // 2, subtract, 0)

    def turn(r):
        for a in range(2):
            for j in range(tiles):
                x = nat[a, pl.ds(j * LANES * rows + r, LANES, stride=rows), :]
                slab[a, j, r, pl.ds(8, LANES), :] = x.T

    turn(0)
    turn(rows - 1)
    pl.semaphore_wait(barrier, nlon - 1 + nlat - 1 + 4)
    lat_copies = []
    for d, (peer, r) in enumerate(((up, 0), (down, rows - 1))):
        copy = pltpu.make_async_remote_copy(
            src_ref=slab.at[:, :, r, pl.ds(8, LANES), :],
            dst_ref=halo.at[1 - d, :, :, pl.ds(8, LANES), :],
            send_sem=lat_send.at[d],
            recv_sem=lat_recv.at[1 - d],
            device_id=(peer, lon),
            device_id_type=MESH,
        )
        copy.start()
        lat_copies.append(copy)

    def turn_rest(r, carry):
        turn(r)
        return carry

    lax.fori_loop(1, rows - 1, turn_rest, 0)

    for s, column in enumerate((8, 7 + LANES)):
        for a in range(2):
            for j in range(tiles):
                side_out[s, :, a * tiles + j, :] = slab[a, j, :, column, :]
    lon_copies = []
    for s, peer in enumerate((left, right)):
        copy = pltpu.make_async_remote_copy(
            src_ref=side_out.at[s],
            dst_ref=side_in.at[1 - s, pl.ds(1, rows)],
            send_sem=lon_send.at[s],
            recv_sem=lon_recv.at[1 - s],
            device_id=(lat, peer),
            device_id_type=MESH,
        )
        copy.start()
        lon_copies.append(copy)
    cor_copies = []
    for n, peer in enumerate(corners):
        v, s = n // 2, n % 2
        copy = pltpu.make_async_remote_copy(
            src_ref=side_out.at[s, 0 if v == 0 else rows - 1],
            dst_ref=side_in.at[1 - s, rows + 1 if v == 0 else 0],
            send_sem=cor_send.at[n],
            recv_sem=cor_recv.at[3 - n],
            device_id=peer,
            device_id_type=MESH,
        )
        copy.start()
        cor_copies.append(copy)

    def across(ref, index, g):
        low = ref[(*index, pl.ds(g * 8 + 7, 8), slice(None))]
        mid = ref[(*index, pl.ds(pl.multiple_of(g * 8 + 8, 8), 8), slice(None))]
        high = ref[(*index, pl.ds(g * 8 + 9, 8), slice(None))]
        return low + mid + high

    def account(acc, j, r, g, fcst, true):
        s0, s1, s2, s3, s4, s5 = acc
        w = weight[r]
        delta = fcst - true
        diff[j, r, pl.ds(pl.multiple_of(g * 8, 8), 8), :] = delta
        wf = w * fcst
        wt = w * true
        return (
            s0 + (w * delta) * delta,
            s1 + wf,
            s2 + wt,
            s3 + wf * fcst,
            s4 + wt * true,
            s5 + wf * true,
        )

    def inner(j, g, acc):
        fa, ta = across(slab, (0, j, 0), g), across(slab, (1, j, 0), g)
        fb, tb = across(slab, (0, j, 1), g), across(slab, (1, j, 1), g)
        for r in range(1, rows - 1):
            fc, tc = across(slab, (0, j, r + 1), g), across(slab, (1, j, r + 1), g)
            acc = account(acc, j, r, g, fa + fb + fc, ta + tb + tc)
            fa, fb, ta, tb = fb, fc, tb, tc
        return acc

    def outer(j, g, acc):
        both = []
        for a in range(2):
            above = across(halo, (0, a, j), g) * north_in
            x = above + across(slab, (a, j, 0), g) + across(slab, (a, j, 1), g)
            both.append(x * north)
        acc = account(acc, j, 0, g, *both)
        both = []
        for a in range(2):
            below = across(halo, (1, a, j), g) * south_in
            x = across(slab, (a, j, rows - 2), g) + across(slab, (a, j, rows - 1), g) + below
            both.append(x * south)
        return account(acc, j, rows - 1, g, *both)

    groups = LANES // 8
    zero = tuple(jnp.zeros((8, LANES), F32) for _ in range(6))
    accs = [
        lax.fori_loop(1, groups - 1, lambda g, acc, j=j: inner(j, g, acc), zero)
        for j in range(tiles)
    ]

    for copy in lon_copies:
        copy.wait_recv()
    for s, column in enumerate((7, 8 + LANES)):
        for a in range(2):
            for j in range(tiles):
                slab[a, j, :, column, :] = side_in[s, pl.ds(1, rows), a * tiles + j, :]
    for j in range(tiles):
        accs[j] = lax.fori_loop(
            0, 2, lambda g, acc, j=j: inner(j, g * (groups - 1), acc), accs[j]
        )

    for copy in lat_copies:
        copy.wait_recv()
    for copy in cor_copies:
        copy.wait_recv()
    for s, column in enumerate((7, 8 + LANES)):
        for v, r in enumerate((0, rows + 1)):
            for a in range(2):
                for j in range(tiles):
                    halo[v, a, j, pl.ds(column, 1), :] = side_in[s, r, pl.ds(a * tiles + j, 1), :]
    for j in range(tiles):
        accs[j] = lax.fori_loop(0, groups, lambda g, acc, j=j: outer(j, g, acc), accs[j])

    for j in range(tiles):
        for n in range(6):
            sums[0, j, pl.ds(n, 1), :] = jnp.sum(accs[j][n], axis=0, keepdims=True)
        sums[0, j, pl.ds(6, 2), :] = jnp.zeros((2, LANES), F32)

    def exchange(stage, me, count, peer_of):
        def send(k):
            return pltpu.make_async_remote_copy(
                src_ref=sums.at[stage],
                dst_ref=got.at[stage, me],
                send_sem=red_send.at[stage, k],
                recv_sem=red_recv.at[stage, me],
                device_id=peer_of(lax.rem(me + k, count)),
                device_id_type=MESH,
            )

        def receive(k):
            who = lax.rem(me + k, count)
            return pltpu.make_async_remote_copy(
                src_ref=sums.at[stage],
                dst_ref=got.at[stage, who],
                send_sem=red_send.at[stage, k],
                recv_sem=red_recv.at[stage, who],
                device_id=peer_of(who),
                device_id_type=MESH,
            )

        def start(k, carry):
            send(k).start()
            return carry

        def finish(k, carry):
            receive(k).wait_recv()
            return carry

        def drain(k, carry):
            send(k).wait_send()
            return carry

        lax.fori_loop(1, count, start, 0)
        got[stage, me] = sums[stage]
        return (
            lambda: lax.fori_loop(1, count, finish, 0),
            lambda: lax.fori_loop(1, count, drain, 0),
        )

    def added(stage, count):
        x = got[stage, 0]
        for k in range(1, count):
            x = x + got[stage, k]
        return x

    arrive0, drain0 = exchange(0, lon, nlon, lambda q: (lat, q))

    def turn_back(r, carry):
        for j in range(tiles):
            x = diff[j, r] * (1.0 / 9.0)
            nat[0, pl.ds(j * LANES * rows + r, LANES, stride=rows), :] = x.T
        return carry

    lax.fori_loop(0, rows // 2, turn_back, 0)
    arrive0()
    sums[1] = added(0, nlon)
    arrive1, drain1 = exchange(1, lat, nlat, lambda q: (q, lon))
    lax.fori_loop(rows // 2, rows, turn_back, 0)

    def narrow(i, carry):
        span = pl.ds(pl.multiple_of(i * step, 16), step)
        out_ref[span, :] = nat[0, span, :].astype(jnp.bfloat16)
        return carry

    lax.fori_loop(0, fields // 2, narrow, 0)
    arrive1()
    tot[...] = added(1, nlat)

    cells = float(total_rows * nlon * LANES)
    for j in range(tiles):
        width = min(LANES, fields - j * LANES)
        s = [tot[j, pl.ds(n, 1), :] for n in range(6)]
        one, two = 1.0 / (9.0 * cells), 1.0 / (81.0 * cells)
        mf, mt = s[1] * one, s[2] * one
        vf = s[3] * two - mf * mf
        vt = s[4] * two - mt * mt
        cv = s[5] * two - mf * mt
        span = pl.ds(j * LANES, width)
        rmse_ref[:, span] = jnp.sqrt(s[0] * two)[:, :width]
        acc_ref[:, span] = (cv / jnp.sqrt((vf + epsilon) * (vt + epsilon)))[:, :width]

    for copy in lat_copies + lon_copies + cor_copies:
        copy.wait_send()
    drain0()
    drain1()


def local(nlat, nlon, predicted_state, observed_state, longterm_average_state):
    fields, rows, columns = predicted_state.shape
    tiles = pl.cdiv(fields, LANES)
    flat = [
        x.reshape(fields * rows, columns)
        for x in (predicted_state, observed_state, longterm_average_state)
    ]
    edges = [2 * (fields // 2 * k // CHUNKS) for k in range(CHUNKS + 1)]
    bounds = tuple((lo, hi) for lo, hi in zip(edges[:-1], edges[1:]) if hi > lo)
    in_vmem = pltpu.VMEM((fields * rows, columns), jnp.bfloat16)
    blurred, rmse, acc = pl.pallas_call(
        functools.partial(kernel, nlat, nlon, fields, rows, bounds),
        out_shape=(
            jax.ShapeDtypeStruct((fields * rows, columns), jnp.bfloat16),
            jax.ShapeDtypeStruct((1, fields), F32),
            jax.ShapeDtypeStruct((1, fields), F32),
        ),
        in_specs=[pl.BlockSpec(memory_space=pltpu.HBM)] * 3,
        out_specs=[pl.BlockSpec(memory_space=pltpu.VMEM)] * 3,
        scratch_shapes=[
            in_vmem, in_vmem, in_vmem,
            pltpu.VMEM((2, tiles * LANES * rows, LANES), F32),
            pltpu.VMEM((2, tiles, rows, LANES + 16, LANES), F32),
            pltpu.VMEM((tiles, rows, LANES, LANES), F32),
            pltpu.VMEM((2, 2, tiles, LANES + 16, LANES), F32),
            pltpu.VMEM((2, rows, 2 * tiles, LANES), F32),
            pltpu.VMEM((2, rows + 2, 2 * tiles, LANES), F32),
            pltpu.VMEM((rows, 8, LANES), F32),
            pltpu.VMEM((2, tiles, 8, LANES), F32),
            pltpu.VMEM((8, LANES), F32),
            pltpu.VMEM((2, max(nlat, nlon), tiles, 8, LANES), F32),
            pltpu.VMEM((tiles, 8, LANES), F32),
            pltpu.SemaphoreType.DMA((CHUNKS, 3)),
            pltpu.SemaphoreType.DMA((2,)),
            pltpu.SemaphoreType.DMA((2,)),
            pltpu.SemaphoreType.DMA((2,)),
            pltpu.SemaphoreType.DMA((2,)),
            pltpu.SemaphoreType.DMA((4,)),
            pltpu.SemaphoreType.DMA((4,)),
            pltpu.SemaphoreType.DMA((2, max(nlat, nlon))),
            pltpu.SemaphoreType.DMA((2, max(nlat, nlon))),
        ],
        compiler_params=pltpu.CompilerParams(
            collective_id=0, has_side_effects=True, vmem_limit_bytes=56 * 1024 * 1024
        ),
    )(*flat)
    return (
        blurred.reshape(fields, rows, columns),
        rmse.reshape(fields),
        acc.reshape(fields),
    )


def solution(mesh):
    placed = (P(None, "lat", "lon"), P(None, "lat", "lon"), P(None, "lat", "lon"))
    return jax.shard_map(
        functools.partial(local, mesh.shape["lat"], mesh.shape["lon"]),
        mesh=mesh,
        in_specs=placed,
        out_specs=(P(None, "lat", "lon"), P(), P()),
        check_vma=False,
    )
```

time: 117 us -> 40.3 us (0.34)
  other arithmetic: 43.8 us -> 0 us
  Pallas kernels: 0 us -> 35 us
  local copies, waits for them, and re-layouts: 24.3 us -> 4.54 us
  blocking collectives: 18.5 us -> 0 us
  starting transfers between devices: 14.9 us -> 0 us
  waiting for transfers between devices: 13.7 us -> 0 us
    pallas_call x0 -> x1, Pallas kernels: none -> 35 us  [local(): pl.pallas_call(functools.partial(kernel, nlat, nlon, fields, rows, bounds...]
    all_to_all x1 -> x0, blocking collectives: 18.5 us -> none  [sent_to_all(): lax.all_to_all(jnp.broadcast_to(x[None], (length, *x.shape)), axis, 0, 0,...]
    unnamed x8 -> x7, local copies, waits for them, and re-layouts: 18.7 us -> 4.54 us
    ppermute x4 -> x0, waiting for transfers between devices: 13.7 us -> none  [the longest x2 7.94 us: extended(): lax.ppermute(head, axis, [((i + 1) % count, i) for i in range(ends)])]
    concatenate x2 -> x0, other arithmetic: 12.6 us -> none  [extended(): jnp.concatenate([lax.ppermute(tail, axis, [(i, (i + 1) % count) for i in...]
    another operation x1 -> x0, other arithmetic: 11.5 us -> none  [local(): jnp.stack([vertical_sum(stretched[0]), vertical_sum(stretched[1])])]
    ppermute x4 -> x0, starting transfers between devices: 9.48 us -> none  [the longest x2 8.2 us: extended(): lax.ppermute(tail, axis, [(i, (i + 1) % count) for i in range(ends)])]
    reduce_sum x4 -> x0, other arithmetic: 7.53 us -> none  [the longest x1 6.83 us: local(): jnp.sum(weighted_fcst * averaged_observation, axis=(1, 2))]
  transfers between devices with their start and end apart: 5 -> 0, of which waited for: 4 -> 0; matrix products, arithmetic and copies ran while one was open for 8% -> 0% of each run, Pallas kernels for 0% -> 0%
where the time goes in v1:
time: 40.3 us; the launch traced here: 40.2 us
  Pallas kernels  35 us (87%)
  local copies, waits for them, and re-layouts  4.54 us (11%)
  between operations  0.66 us (2%)
    pallas_call x1, Pallas kernels, local(): pl.pallas_call(functools.partial(kernel, nlat, nlon, fields, rows, bounds...  35 us
    unnamed x7, local copies, waits for them, and re-layouts  4.54 us

profile of v1, /device:TPU:1, one launch (start us, length us, event | category | flops | bytes accessed | tf_op | source)
XLA Modules:
  0.0 40.2 jit_solution(12372627588956914798)
XLA Ops:
  0.6 35.0 %shard_map.58 = (bf16[8880,128]{1,0:T(8,128)(2,1)}, f32[1,222]{1,0:T(1,128)}, f32[1,222]{1,0:T(1,128)}) custom-call(bf16[8880,128]{1,0:T(8,128)(2,1)} %bitcast.6, bf16[8880,128]{1,0:T(8,128)(2,1)} %bitcast.7, bf16[8880,128]{1,0:T(8,128)(2,1)} %bitcast.8), custom_call_target="tpu_custom_call" | custom-call | tf_op jit(solution)/shard_map/pallas_call | solution.py:334
  35.7 0.0 copy-start.1
  35.7 0.0 copy-start
  35.7 3.4 %copy.9 = bf16[222,40,128]{2,1,0:T(8,128)(2,1)} copy(bf16[222,40,128]{2,1,0:T(8,128)(2,1)} %bitcast.9) | data formatting | bytes 4546560
  39.1 0.0 copy-done.1
  39.1 0.6 %copy.10 = f32[222]{0:T(256)} copy(f32[222]{0:T(256)S(1)} %bitcast.11) | data formatting | bytes 1776
  39.6 0.0 copy-done
  39.6 0.6 %copy.11 = f32[222]{0:T(256)} copy(f32[222]{0:T(256)S(1)} %bitcast.10) | data formatting | bytes 1776
Async XLA Ops:
  35.7 3.4 %copy-start.1 = (f32[1,222]{1,0:T(1,128)S(1)}, f32[1,222]{1,0:T(1,128)}, u32[]{:S(2)}) copy-start(f32[1,222]{1,0:T(1,128)} %get-tuple-element.7) | copy-start | bytes 2668
  35.7 4.0 %copy-start = (f32[1,222]{1,0:T(1,128)S(1)}, f32[1,222]{1,0:T(1,128)}, u32[]{:S(2)}) copy-start(f32[1,222]{1,0:T(1,128)} %get-tuple-element.8) | copy-start | bytes 2668

commit v2 on v1

--- a/solution.py
+++ b/solution.py
@@ -13,7 +13,8 @@
 MESH = pl.DeviceIdType.MESH
 F32 = jnp.float32
 LANES = 128
-CHUNKS = 8
+STEP = 8
+CHUNK = 32
 
 
 def mean_cosine(rows):
@@ -25,7 +26,8 @@
     nlat, nlon, fields, rows, bounds,
     p_hbm, o_hbm, c_hbm,
     out_ref, rmse_ref, acc_ref,
-    p, o, c, nat, slab, diff, halo, side_out, side_in, weight, sums, part, got, tot,
+    p, o, c, nat, slab, diff, halo, edge, edge_out, edge_in, side_out, side_in,
+    weight, sums, got, tot,
     in_sem, lat_send, lat_recv, lon_send, lon_recv, cor_send, cor_recv, red_send, red_recv,
 ):
     lat = lax.axis_index("lat")
@@ -37,6 +39,41 @@
     tiles = slab.shape[1]
     total_rows = nlat * rows
 
+    depth, width = nlat // 2, nlon // 4
+    z, y_hi = lax.rem(lat, depth), lat // depth
+    core, y_lo, x = lax.rem(lon, 2), lax.rem(lon // 2, 2), lon // 4
+    y = y_hi * 2 + y_lo
+
+    def place(px, py, pz, pc):
+        return ((py // 2) * depth + pz, (px * 2 + lax.rem(py, 2)) * 2 + pc)
+
+    def ring(a, b, n):
+        return min((a - b) % n, (b - a) % n)
+
+    plane = sorted(
+        ((dx, dy) for dx in range(width) for dy in range(4) if dx or dy),
+        key=lambda q: -ring(q[0], 0, width) - ring(q[1], 0, 4),
+    )
+    line = sorted(
+        ((dz, dc) for dz in range(depth) for dc in range(2) if dz or dc),
+        key=lambda q: -ring(q[0], 0, depth) - 0.5 * q[1],
+    )
+    plane_peers = []
+    for dx, dy in plane:
+        px, py = lax.rem(x + dx, width), lax.rem(y + dy, 4)
+        plane_peers.append((place(px, py, z, core), px * 4 + py))
+    line_peers = []
+    for dz, dc in line:
+        pz, pc = lax.rem(z + dz, depth), lax.rem(core + dc, 2)
+        line_peers.append((place(x, y, pz, pc), pz * 2 + pc))
+    corners = ((up, left), (up, right), (down, left), (down, right))
+    sides = ((up, lon), (down, lon), (lat, left), (lat, right))
+
+    barrier = pltpu.get_barrier_semaphore()
+    greeted = [q[0] for q in line_peers + plane_peers] + list(sides) + list(corners)
+    for peer in greeted:
+        pl.semaphore_signal(barrier, inc=1, device_id=peer, device_id_type=MESH)
+
     loads = []
     for k, (lo, hi) in enumerate(bounds):
         span = pl.ds(lo * rows, (hi - lo) * rows)
@@ -48,26 +85,6 @@
             copy.start()
         loads.append(group)
 
-    barrier = pltpu.get_barrier_semaphore()
-
-    def greet_lon(k, carry):
-        pl.semaphore_signal(
-            barrier, inc=1, device_id=(lat, lax.rem(lon + k, nlon)), device_id_type=MESH
-        )
-        return carry
-
-    def greet_lat(k, carry):
-        pl.semaphore_signal(
-            barrier, inc=1, device_id=(lax.rem(lat + k, nlat), lon), device_id_type=MESH
-        )
-        return carry
-
-    corners = ((up, left), (up, right), (down, left), (down, right))
-    for peer in corners:
-        pl.semaphore_signal(barrier, inc=1, device_id=peer, device_id_type=MESH)
-    lax.fori_loop(1, nlon, greet_lon, 0)
-    lax.fori_loop(1, nlat, greet_lat, 0)
-
     row = (lax.broadcasted_iota(jnp.int32, (rows, 8, LANES), 0) + lat * rows).astype(F32)
     cosine = jnp.cos(jnp.pi * (0.5 - row / (total_rows - 1)))
     weight[...] = cosine * (1.0 / mean_cosine(total_rows))
@@ -80,47 +97,73 @@
     if padded > fields * rows:
         for a in range(2):
             nat[a, fields * rows :, :] = jnp.zeros((padded - fields * rows, LANES), F32)
-    step = 2 * rows
-    for k, (lo, hi) in enumerate(bounds):
+    edge[:, :, fields:, :] = jnp.zeros((2, 3, edge.shape[2] - fields, LANES), F32)
+
+    def subtract(first, count):
+        start = first * rows
+        if not isinstance(start, int):
+            start = pl.multiple_of(start, 16)
+        span = pl.ds(start, count * rows)
+        three = [src[span, :].astype(F32) for src in (p, o, c)]
+        nat[0, span, :] = three[0] - three[2]
+        nat[1, span, :] = three[1] - three[2]
+        for n in range(3):
+            for q in range(count):
+                for v, r in enumerate((0, rows - 1)):
+                    at = q * rows + r
+                    edge[v, n, pl.ds(first + q, 1), :] = three[n][at : at + 1, :]
+
+    def subtract_chunk(k):
+        lo, hi = bounds[k]
         for copy in loads[k]:
             copy.wait()
-
-        def subtract(i, carry):
-            span = pl.ds(pl.multiple_of(i * step, 16), step)
-            normal = c[span, :].astype(F32)
-            nat[0, span, :] = p[span, :].astype(F32) - normal
-            nat[1, span, :] = o[span, :].astype(F32) - normal
+        whole = (hi - lo) // STEP
+
+        def body(i, carry):
+            subtract(lo + i * STEP, STEP)
             return carry
 
-        lax.fori_loop(lo // 2, hi // 2, subtract, 0)
-
-    def turn(r):
-        for a in range(2):
-            for j in range(tiles):
-                x = nat[a, pl.ds(j * LANES * rows + r, LANES, stride=rows), :]
-                slab[a, j, r, pl.ds(8, LANES), :] = x.T
-
-    turn(0)
-    turn(rows - 1)
-    pl.semaphore_wait(barrier, nlon - 1 + nlat - 1 + 4)
+        lax.fori_loop(0, whole, body, 0)
+        if lo + whole * STEP < hi:
+            subtract(lo + whole * STEP, hi - lo - whole * STEP)
+
+    def turn(j, r):
+        for a in range(2):
+            t = nat[a, pl.ds(j * LANES * rows + r, LANES, stride=rows), :]
+            slab[a, j, r, pl.ds(8, LANES), :] = t.T
+
+    def turn_all(j):
+        def body(i, carry):
+            for k in range(rows // 2):
+                turn(j, i * (rows // 2) + k)
+            return carry
+
+        lax.fori_loop(0, 2, body, 0)
+
+    for j in range(tiles):
+        for k, (lo, hi) in enumerate(bounds):
+            if lo // LANES == j:
+                subtract_chunk(k)
+        if j < tiles - 1:
+            turn_all(j)
+
+    for v in range(2):
+        for n in range(3):
+            edge_out[v, n] = edge[v, n].astype(jnp.bfloat16)
+    pl.semaphore_wait(barrier, len(greeted))
     lat_copies = []
-    for d, (peer, r) in enumerate(((up, 0), (down, rows - 1))):
+    for v, peer in enumerate((up, down)):
         copy = pltpu.make_async_remote_copy(
-            src_ref=slab.at[:, :, r, pl.ds(8, LANES), :],
-            dst_ref=halo.at[1 - d, :, :, pl.ds(8, LANES), :],
-            send_sem=lat_send.at[d],
-            recv_sem=lat_recv.at[1 - d],
+            src_ref=edge_out.at[v],
+            dst_ref=edge_in.at[1 - v],
+            send_sem=lat_send.at[v],
+            recv_sem=lat_recv.at[1 - v],
             device_id=(peer, lon),
             device_id_type=MESH,
         )
         copy.start()
         lat_copies.append(copy)
-
-    def turn_rest(r, carry):
-        turn(r)
-        return carry
-
-    lax.fori_loop(1, rows - 1, turn_rest, 0)
+    turn_all(tiles - 1)
 
     for s, column in enumerate((8, 7 + LANES)):
         for a in range(2):
@@ -217,6 +260,12 @@
 
     for copy in lat_copies:
         copy.wait_recv()
+    for v in range(2):
+        normal = edge_in[v, 2].astype(F32)
+        for a in range(2):
+            t = edge_in[v, a].astype(F32) - normal
+            for j in range(tiles):
+                halo[v, a, j, pl.ds(8, LANES), :] = t[j * LANES : (j + 1) * LANES, :].T
     for copy in cor_copies:
         copy.wait_recv()
     for s, column in enumerate((7, 8 + LANES)):
@@ -229,49 +278,32 @@
 
     for j in range(tiles):
         for n in range(6):
-            sums[0, j, pl.ds(n, 1), :] = jnp.sum(accs[j][n], axis=0, keepdims=True)
-        sums[0, j, pl.ds(6, 2), :] = jnp.zeros((2, LANES), F32)
-
-    def exchange(stage, me, count, peer_of):
-        def send(k):
+            sums[0, pl.ds(n * tiles + j, 1), :] = jnp.sum(accs[j][n], axis=0, keepdims=True)
+
+    def exchange(stage, me, peers):
+        def copy_of(k, slot):
             return pltpu.make_async_remote_copy(
                 src_ref=sums.at[stage],
-                dst_ref=got.at[stage, me],
+                dst_ref=got.at[stage, slot],
                 send_sem=red_send.at[stage, k],
-                recv_sem=red_recv.at[stage, me],
-                device_id=peer_of(lax.rem(me + k, count)),
+                recv_sem=red_recv.at[stage, slot],
+                device_id=peers[k][0],
                 device_id_type=MESH,
             )
 
-        def receive(k):
-            who = lax.rem(me + k, count)
-            return pltpu.make_async_remote_copy(
-                src_ref=sums.at[stage],
-                dst_ref=got.at[stage, who],
-                send_sem=red_send.at[stage, k],
-                recv_sem=red_recv.at[stage, who],
-                device_id=peer_of(who),
-                device_id_type=MESH,
-            )
-
-        def start(k, carry):
-            send(k).start()
-            return carry
-
-        def finish(k, carry):
-            receive(k).wait_recv()
-            return carry
-
-        def drain(k, carry):
-            send(k).wait_send()
-            return carry
-
-        lax.fori_loop(1, count, start, 0)
+        for k in range(len(peers)):
+            copy_of(k, me).start()
         got[stage, me] = sums[stage]
-        return (
-            lambda: lax.fori_loop(1, count, finish, 0),
-            lambda: lax.fori_loop(1, count, drain, 0),
-        )
+
+        def arrive():
+            for k, (_, who) in enumerate(peers):
+                copy_of(k, who).wait_recv()
+
+        def drain():
+            for k in range(len(peers)):
+                copy_of(k, me).wait_send()
+
+        return arrive, drain
 
     def added(stage, count):
         x = got[stage, 0]
@@ -279,41 +311,48 @@
             x = x + got[stage, k]
         return x
 
-    arrive0, drain0 = exchange(0, lon, nlon, lambda q: (lat, q))
+    arrive0, drain0 = exchange(0, x * 4 + y, plane_peers)
 
     def turn_back(r, carry):
         for j in range(tiles):
-            x = diff[j, r] * (1.0 / 9.0)
-            nat[0, pl.ds(j * LANES * rows + r, LANES, stride=rows), :] = x.T
+            t = diff[j, r] * (1.0 / 9.0)
+            nat[0, pl.ds(j * LANES * rows + r, LANES, stride=rows), :] = t.T
         return carry
 
     lax.fori_loop(0, rows // 2, turn_back, 0)
     arrive0()
-    sums[1] = added(0, nlon)
-    arrive1, drain1 = exchange(1, lat, nlat, lambda q: (q, lon))
+    sums[1] = added(0, len(plane_peers) + 1)
+    arrive1, drain1 = exchange(1, z * 2 + core, line_peers)
     lax.fori_loop(rows // 2, rows, turn_back, 0)
 
-    def narrow(i, carry):
-        span = pl.ds(pl.multiple_of(i * step, 16), step)
+    def narrow(start, count):
+        span = pl.ds(start, count * rows)
         out_ref[span, :] = nat[0, span, :].astype(jnp.bfloat16)
+
+    def narrow_step(i, carry):
+        narrow(pl.multiple_of(i * (STEP * rows), 16), STEP)
         return carry
 
-    lax.fori_loop(0, fields // 2, narrow, 0)
+    lax.fori_loop(0, fields // STEP, narrow_step, 0)
+    if fields % STEP:
+        narrow(fields // STEP * STEP * rows, fields % STEP)
     arrive1()
-    tot[...] = added(1, nlat)
+    tot[...] = added(1, len(line_peers) + 1)
 
     cells = float(total_rows * nlon * LANES)
+    s = [tot[pl.ds(n * tiles, tiles), :] for n in range(6)]
+    one, two = 1.0 / (9.0 * cells), 1.0 / (81.0 * cells)
+    mf, mt = s[1] * one, s[2] * one
+    vf = s[3] * two - mf * mf
+    vt = s[4] * two - mt * mt
+    cv = s[5] * two - mf * mt
+    rmse = jnp.sqrt(s[0] * two)
+    acc = cv / jnp.sqrt((vf + epsilon) * (vt + epsilon))
     for j in range(tiles):
-        width = min(LANES, fields - j * LANES)
-        s = [tot[j, pl.ds(n, 1), :] for n in range(6)]
-        one, two = 1.0 / (9.0 * cells), 1.0 / (81.0 * cells)
-        mf, mt = s[1] * one, s[2] * one
-        vf = s[3] * two - mf * mf
-        vt = s[4] * two - mt * mt
-        cv = s[5] * two - mf * mt
-        span = pl.ds(j * LANES, width)
-        rmse_ref[:, span] = jnp.sqrt(s[0] * two)[:, :width]
-        acc_ref[:, span] = (cv / jnp.sqrt((vf + epsilon) * (vt + epsilon)))[:, :width]
+        width_j = min(LANES, fields - j * LANES)
+        span = pl.ds(j * LANES, width_j)
+        rmse_ref[:, span] = rmse[j : j + 1, :width_j]
+        acc_ref[:, span] = acc[j : j + 1, :width_j]
 
     for copy in lat_copies + lon_copies + cor_copies:
         copy.wait_send()
@@ -328,8 +367,10 @@
         x.reshape(fields * rows, columns)
         for x in (predicted_state, observed_state, longterm_average_state)
     ]
-    edges = [2 * (fields // 2 * k // CHUNKS) for k in range(CHUNKS + 1)]
-    bounds = tuple((lo, hi) for lo, hi in zip(edges[:-1], edges[1:]) if hi > lo)
+    edges = list(range(0, fields, CHUNK)) + [fields]
+    bounds = tuple(zip(edges[:-1], edges[1:]))
+    field_rows = tiles * LANES
+    group = max(nlat, nlon)
     in_vmem = pltpu.VMEM((fields * rows, columns), jnp.bfloat16)
     blurred, rmse, acc = pl.pallas_call(
         functools.partial(kernel, nlat, nlon, fields, rows, bounds),
@@ -346,25 +387,27 @@
             pltpu.VMEM((2, tiles, rows, LANES + 16, LANES), F32),
             pltpu.VMEM((tiles, rows, LANES, LANES), F32),
             pltpu.VMEM((2, 2, tiles, LANES + 16, LANES), F32),
+            pltpu.VMEM((2, 3, field_rows, LANES), F32),
+            pltpu.VMEM((2, 3, field_rows, LANES), jnp.bfloat16),
+            pltpu.VMEM((2, 3, field_rows, LANES), jnp.bfloat16),
             pltpu.VMEM((2, rows, 2 * tiles, LANES), F32),
             pltpu.VMEM((2, rows + 2, 2 * tiles, LANES), F32),
             pltpu.VMEM((rows, 8, LANES), F32),
-            pltpu.VMEM((2, tiles, 8, LANES), F32),
-            pltpu.VMEM((8, LANES), F32),
-            pltpu.VMEM((2, max(nlat, nlon), tiles, 8, LANES), F32),
-            pltpu.VMEM((tiles, 8, LANES), F32),
-            pltpu.SemaphoreType.DMA((CHUNKS, 3)),
+            pltpu.VMEM((2, 6 * tiles, LANES), F32),
+            pltpu.VMEM((2, group, 6 * tiles, LANES), F32),
+            pltpu.VMEM((6 * tiles, LANES), F32),
+            pltpu.SemaphoreType.DMA((len(bounds), 3)),
             pltpu.SemaphoreType.DMA((2,)),
             pltpu.SemaphoreType.DMA((2,)),
             pltpu.SemaphoreType.DMA((2,)),
             pltpu.SemaphoreType.DMA((2,)),
             pltpu.SemaphoreType.DMA((4,)),
             pltpu.SemaphoreType.DMA((4,)),
-            pltpu.SemaphoreType.DMA((2, max(nlat, nlon))),
-            pltpu.SemaphoreType.DMA((2, max(nlat, nlon))),
+            pltpu.SemaphoreType.DMA((2, group)),
+            pltpu.SemaphoreType.DMA((2, group)),
         ],
         compiler_params=pltpu.CompilerParams(
-            collective_id=0, has_side_effects=True, vmem_limit_bytes=56 * 1024 * 1024
+            collective_id=0, has_side_effects=True, vmem_limit_bytes=50 * 1024 * 1024
         ),
     )(*flat)
     return (

time: 40.3 us -> 33.6 us (0.83)
  Pallas kernels: 35 us -> 30.4 us
  local copies, waits for them, and re-layouts: 4.54 us -> 2.5 us
    pallas_call x1, Pallas kernels: 35 us -> 30.4 us  [local(): pl.pallas_call(functools.partial(kernel, nlat, nlon, fields, rows, bounds...]
    unnamed x7 -> x3, local copies, waits for them, and re-layouts: 4.54 us -> 2.5 us
where the time goes in v2:
time: 33.6 us
  Pallas kernels  30.4 us (90%)
  local copies, waits for them, and re-layouts  2.5 us (7%)
  between operations  0.64 us (2%)
    pallas_call x1, Pallas kernels, local(): pl.pallas_call(functools.partial(kernel, nlat, nlon, fields, rows, bounds...  30.4 us
    unnamed x3, local copies, waits for them, and re-layouts  2.5 us

profile of v2, /device:TPU:1, one launch (start us, length us, event | category | flops | bytes accessed | tf_op | source)
XLA Modules:
  0.0 33.6 jit_solution(5882239169622834992)
XLA Ops:
  0.6 30.4 %shard_map.58 = (bf16[8880,128]{1,0:T(8,128)(2,1)S(1)}, f32[1,222]{1,0:T(1,128)S(1)}, f32[1,222]{1,0:T(1,128)S(1)}) custom-call(bf16[8880,128]{1,0:T(8,128)(2,1)} %bitcast.9, bf16[8880,128]{1,0:T(8,128)(2,1)} %bitcast.10, bf16[8880,128]{1,0:T(8,128)(2,1)} %bitcast.11), custom_call_target="tpu_custom_call" | custom-call | tf_op jit(solution)/shard_map/pallas_call | solution.py:375
  31.0 1.4 %copy.9 = bf16[222,40,128]{2,1,0:T(8,128)(2,1)} copy(bf16[222,40,128]{2,1,0:T(8,128)(2,1)S(1)} %bitcast.6) | data formatting | bytes 4546560
  32.4 0.6 %copy.10 = f32[222]{0:T(256)} copy(f32[222]{0:T(256)S(1)} %bitcast.8) | data formatting | bytes 1776
  33.0 0.6 %copy.11 = f32[222]{0:T(256)} copy(f32[222]{0:T(256)S(1)} %bitcast.7) | data formatting | bytes 1776

commit v3 on v2

v3 whole, which is shorter than its diff:
```python
import functools
import math

import jax
import jax.numpy as jnp
import numpy as np
from jax import lax
from jax.experimental import pallas as pl
from jax.experimental.pallas import tpu as pltpu
from jax.sharding import PartitionSpec as P

MESH = pl.DeviceIdType.MESH
F32 = jnp.float32
LANES = 128
STEP = 8
AT_ONCE = 7
CHUNK = 64


def mean_cosine(rows):
    i = np.arange(rows, dtype=np.float64)
    return float(np.mean(np.cos(np.pi * (0.5 - i / (rows - 1)))))


def kernel(
    nlat, nlon, fields, rows, bounds,
    p_hbm, o_hbm, c_hbm,
    out_ref, tot_ref,
    p, o, c, nat0, nat1, slab0, slab1, diff, halo, edge, edge_out, edge_in, side_out, side_in,
    pairs, weight, sums, got,
    in_sem, lat_send, lat_recv, lon_send, lon_recv, cor_send, cor_recv, red_send, red_recv,
):
    lat = lax.axis_index("lat")
    lon = lax.axis_index("lon")
    up = lax.rem(lat + nlat - 1, nlat)
    down = lax.rem(lat + 1, nlat)
    left = lax.rem(lon + nlon - 1, nlon)
    right = lax.rem(lon + 1, nlon)
    tiles = 2
    pitch = rows + 1
    nat, slab = (nat0, nat1), (slab0, slab1)
    total_rows = nlat * rows

    loads = []
    for k, (lo, hi) in enumerate(bounds):
        span = pl.ds(lo * rows, (hi - lo) * rows)
        group = [
            pltpu.make_async_copy(src.at[span, :], dst.at[span, :], in_sem.at[k, n])
            for n, (src, dst) in enumerate(((p_hbm, p), (o_hbm, o), (c_hbm, c)))
        ]
        for copy in group:
            copy.start()
        loads.append(group)

    depth, width = nlat // 2, nlon // 4
    z, y_hi = lax.rem(lat, depth), lat // depth
    core, y_lo, x = lax.rem(lon, 2), lax.rem(lon // 2, 2), lon // 4
    y = y_hi * 2 + y_lo

    def place(px, py, pz, pc):
        return ((py // 2) * depth + pz, (px * 2 + lax.rem(py, 2)) * 2 + pc)

    def ring(a, b, n):
        return min((a - b) % n, (b - a) % n)

    plane = sorted(
        ((dx, dy) for dx in range(width) for dy in range(4) if dx or dy),
        key=lambda q: -ring(q[0], 0, width) - ring(q[1], 0, 4),
    )
    line = sorted(
        ((dz, dc) for dz in range(depth) for dc in range(2) if dz or dc),
        key=lambda q: -ring(q[0], 0, depth) - 0.5 * q[1],
    )
    plane_peers = []
    for dx, dy in plane:
        px, py = lax.rem(x + dx, width), lax.rem(y + dy, 4)
        plane_peers.append((place(px, py, z, core), px * 4 + py))
    line_peers = []
    for dz, dc in line:
        pz, pc = lax.rem(z + dz, depth), lax.rem(core + dc, 2)
        line_peers.append((place(x, y, pz, pc), pz * 2 + pc))
    corners = ((up, left), (up, right), (down, left), (down, right))
    sides = ((up, lon), (down, lon), (lat, left), (lat, right))

    barrier = pltpu.get_barrier_semaphore()
    greeted = [q[0] for q in line_peers + plane_peers] + list(sides) + list(corners)
    for peer in greeted:
        pl.semaphore_signal(barrier, inc=1, device_id=peer, device_id_type=MESH)

    row = (lax.broadcasted_iota(jnp.int32, (rows, 8, LANES), 0) + lat * rows).astype(F32)
    cosine = jnp.cos(jnp.pi * (0.5 - row / (total_rows - 1)))
    weight[...] = cosine * (1.0 / mean_cosine(total_rows))
    north = jnp.where(lat == 0, 1.5, 1.0).astype(F32)
    south = jnp.where(lat == nlat - 1, 1.5, 1.0).astype(F32)
    north_in = jnp.where(lat == 0, 0.0, 1.0).astype(F32)
    south_in = jnp.where(lat == nlat - 1, 0.0, 1.0).astype(F32)

    rest = tiles * LANES - fields
    if rest:
        for a in range(2):
            nat1[a, pl.ds((LANES - rest) // 8 * 8 * pitch, (rest + 7) // 8 * 8 * pitch), :] = (
                jnp.zeros(((rest + 7) // 8 * 8 * pitch, LANES), F32)
            )
    if edge.shape[2] > fields:
        edge[:, :, fields:, :] = jnp.zeros((2, 3, edge.shape[2] - fields, LANES), F32)

    def subtract(j, first, count):
        span = pl.ds(pl.multiple_of(first * rows, 16), count * rows)
        three = [src[span, :].astype(F32) for src in (p, o, c)]
        for q in range(count):
            into = pl.ds((first + q - j * LANES) * pitch, rows)
            normal = three[2][q * rows : (q + 1) * rows]
            for a in range(2):
                nat[j][a, into, :] = three[a][q * rows : (q + 1) * rows] - normal
        for n in range(3):
            for q in range(count):
                for v, r in enumerate((0, rows - 1)):
                    at = q * rows + r
                    edge[v, n, pl.ds(first + q, 1), :] = three[n][at : at + 1, :]

    def subtract_chunk(j, lo, hi):
        whole = (hi - lo) // STEP

        def body(i, carry):
            subtract(j, lo + i * STEP, STEP)
            return carry

        lax.fori_loop(0, whole, body, 0)

        def pair(i, carry):
            subtract(j, lo + whole * STEP + 2 * i, 2)
            return carry

        if lo + whole * STEP < hi:
            lax.fori_loop(0, (hi - lo - whole * STEP) // 2, pair, 0)

    def turn(j, r):
        for a in range(2):
            t = nat[j][a, pl.ds(r, LANES, stride=pitch), :]
            slab[j][a, r, pl.ds(8, LANES), :] = t.T

    for k, (lo, hi) in enumerate(bounds):
        if lo >= LANES:
            break
        for copy in loads[k]:
            copy.wait()

        subtract_chunk(0, lo, hi)

    def turn_rows(lo, hi):
        for r in range(lo, hi):
            turn(0, r)

    turn_rows(0, rows // 2)
    for k, (lo, hi) in enumerate(bounds):
        if lo >= LANES:
            for copy in loads[k]:
                copy.wait()
            subtract_chunk(1, lo, hi)

    for v in range(2):
        for n in range(3):
            edge_out[v, n] = edge[v, n].astype(jnp.bfloat16)
    pl.semaphore_wait(barrier, len(greeted))
    lat_copies = []
    for v, peer in enumerate((up, down)):
        copy = pltpu.make_async_remote_copy(
            src_ref=edge_out.at[v],
            dst_ref=edge_in.at[1 - v],
            send_sem=lat_send.at[v],
            recv_sem=lat_recv.at[1 - v],
            device_id=(peer, lon),
            device_id_type=MESH,
        )
        copy.start()
        lat_copies.append(copy)
    turn_rows(rows // 2, rows)

    def send_columns(j):
        copies = []
        for s, peer in enumerate((left, right)):
            column = 8 if s == 0 else 7 + LANES
            for a in range(2):
                side_out[j, s, :, a, :] = slab[j][a, :, column, :]
        for s, peer in enumerate((left, right)):
            copies.append(
                pltpu.make_async_remote_copy(
                    src_ref=side_out.at[j, s],
                    dst_ref=side_in.at[j, 1 - s, pl.ds(1, rows)],
                    send_sem=lon_send.at[j, s],
                    recv_sem=lon_recv.at[j, 1 - s],
                    device_id=(lat, peer),
                    device_id_type=MESH,
                )
            )
        for n, peer in enumerate(corners):
            v, s = n // 2, n % 2
            copies.append(
                pltpu.make_async_remote_copy(
                    src_ref=side_out.at[j, s, 0 if v == 0 else rows - 1],
                    dst_ref=side_in.at[j, 1 - s, rows + 1 if v == 0 else 0],
                    send_sem=cor_send.at[j, n],
                    recv_sem=cor_recv.at[j, 3 - n],
                    device_id=peer,
                    device_id_type=MESH,
                )
            )
        for copy in copies:
            copy.start()
        return copies[:2], copies[2:]

    def take_columns(j):
        for s, column in enumerate((7, 8 + LANES)):
            for a in range(2):
                slab[j][a, :, column, :] = side_in[j, s, pl.ds(1, rows), a, :]

    def across(ref, index, g):
        low = ref[(*index, pl.ds(g * 8 + 7, 8), slice(None))]
        mid = ref[(*index, pl.ds(pl.multiple_of(g * 8 + 8, 8), 8), slice(None))]
        high = ref[(*index, pl.ds(g * 8 + 9, 8), slice(None))]
        return low + mid + high

    def account(acc, j, r, g, fcst, true):
        s0, s1, s2, s3, s4, s5 = acc
        w = weight[r]
        delta = fcst - true
        diff[j, r, pl.ds(pl.multiple_of(g * 8, 8), 8), :] = delta
        wf = w * fcst
        wt = w * true
        return (
            s0 + (w * delta) * delta,
            s1 + wf,
            s2 + wt,
            s3 + wf * fcst,
            s4 + wt * true,
            s5 + wf * true,
        )

    def inner(j, g, acc):
        fa, ta = across(slab[j], (0, 0), g), across(slab[j], (1, 0), g)
        fb, tb = across(slab[j], (0, 1), g), across(slab[j], (1, 1), g)
        at = pl.ds(pl.multiple_of(g * 8, 8), 8)
        pairs[0, 0, j, at, :], pairs[0, 1, j, at, :] = fa + fb, ta + tb
        for r in range(1, rows - 1):
            fc, tc = across(slab[j], (0, r + 1), g), across(slab[j], (1, r + 1), g)
            acc = account(acc, j, r, g, fa + fb + fc, ta + tb + tc)
            fa, fb, ta, tb = fb, fc, tb, tc
        pairs[1, 0, j, at, :], pairs[1, 1, j, at, :] = fa + fb, ta + tb
        return acc

    def outer(j, g, acc):
        at = pl.ds(pl.multiple_of(g * 8, 8), 8)
        for v, (r, inside, scale) in enumerate(
            ((0, north_in, north), (rows - 1, south_in, south))
        ):
            both = [
                (across(halo, (v, a, j), g) * inside + pairs[v, a, j, at, :]) * scale
                for a in range(2)
            ]
            acc = account(acc, j, r, g, *both)
        return acc

    groups = LANES // 8
    zero = tuple(jnp.zeros((8, LANES), F32) for _ in range(6))
    share = pl.cdiv(rows, groups - 2)

    def mixed(i, acc):
        for q in range(AT_ONCE):
            acc = inner(0, i * AT_ONCE + q + 1, acc)
        for k in range(AT_ONCE * share):
            turn(1, jnp.minimum(i * (AT_ONCE * share) + k, rows - 1))
        return acc

    accs = [None, None]
    lon_copies, cor_copies = [None, None], [None, None]
    lon_copies[0], cor_copies[0] = send_columns(0)
    accs[0] = lax.fori_loop(0, (groups - 2) // AT_ONCE, mixed, zero)
    lon_copies[1], cor_copies[1] = send_columns(1)
    accs[1] = lax.fori_loop(1, groups - 1, lambda g, acc: inner(1, g, acc), zero)

    for j in range(tiles):
        for copy in lon_copies[j]:
            copy.wait_recv()
        take_columns(j)
        accs[j] = lax.fori_loop(
            0, 2, lambda g, acc, j=j: inner(j, g * (groups - 1), acc), accs[j]
        )

    for copy in lat_copies:
        copy.wait_recv()
    tail = edge_in.shape[2] - LANES
    for v in range(2):
        normal = edge_in[v, 2].astype(F32)
        for a in range(2):
            t = edge_in[v, a].astype(F32) - normal
            t = jnp.concatenate([t, jnp.zeros((LANES - tail, LANES), F32)], axis=0)
            for j in range(tiles):
                halo[v, a, j, pl.ds(8, LANES), :] = t[j * LANES : (j + 1) * LANES, :].T
    for j in range(tiles):
        for copy in cor_copies[j]:
            copy.wait_recv()
        for s, column in enumerate((7, 8 + LANES)):
            for v, r in enumerate((0, rows + 1)):
                for a in range(2):
                    halo[v, a, j, pl.ds(column, 1), :] = side_in[j, s, r, pl.ds(a, 1), :]

        def outer_four(i, acc, j=j):
            for q in range(4):
                acc = outer(j, i * 4 + q, acc)
            return acc

        accs[j] = lax.fori_loop(0, groups // 4, outer_four, accs[j])

    for j in range(tiles):
        for n in range(6):
            sums[0, pl.ds(n * tiles + j, 1), :] = jnp.sum(accs[j][n], axis=0, keepdims=True)

    def exchange(stage, me, peers):
        def copy_of(k, slot):
            return pltpu.make_async_remote_copy(
                src_ref=sums.at[stage],
                dst_ref=got.at[stage, slot],
                send_sem=red_send.at[stage, k],
                recv_sem=red_recv.at[stage, slot],
                device_id=peers[k][0],
                device_id_type=MESH,
            )

        for k in range(len(peers)):
            copy_of(k, me).start()
        got[stage, me] = sums[stage]

        def arrive():
            for k, (_, who) in enumerate(peers):
                copy_of(k, who).wait_recv()

        def drain():
            for k in range(len(peers)):
                copy_of(k, me).wait_send()

        return arrive, drain

    def added(stage, count):
        x = got[stage, 0]
        for k in range(1, count):
            x = x + got[stage, k]
        return x

    arrive0, drain0 = exchange(0, x * 4 + y, plane_peers)

    def turn_back(r, carry):
        for j in range(tiles):
            t = diff[j, r] * (1.0 / 9.0)
            nat[j][0, pl.ds(r, LANES, stride=pitch), :] = t.T
        return carry

    lax.fori_loop(0, rows // 2, turn_back, 0)
    arrive0()
    sums[1] = added(0, len(plane_peers) + 1)
    arrive1, drain1 = exchange(1, z * 2 + core, line_peers)
    lax.fori_loop(rows // 2, rows, turn_back, 0)

    for j in range(tiles):
        first, count = j * LANES, min(LANES, fields - j * LANES)

        def narrow(i, carry, j=j, first=first):
            for q in range(2):
                f = 2 * i + q
                out_ref[pl.ds(pl.multiple_of((first + f) * rows, 8), rows), :] = nat[j][
                    0, pl.ds(f * pitch, rows), :
                ].astype(jnp.bfloat16)
            return carry

        lax.fori_loop(0, count // 2, narrow, 0)
    arrive1()
    tot_ref[...] = added(1, len(line_peers) + 1)

    for copy in lat_copies + sum(lon_copies + cor_copies, []):
        copy.wait_send()
    drain0()
    drain1()


def finish(cells, fields, map_ref, tot_ref, out_hbm, rmse_hbm, acc_hbm, rmse_ref, acc_ref, sem):
    tiles = 2
    epsilon = 1e-06
    copy = pltpu.make_async_copy(map_ref, out_hbm, sem.at[0])
    copy.start()
    s = [tot_ref[pl.ds(n * tiles, tiles), :] for n in range(6)]
    one, two = 1.0 / (9.0 * cells), 1.0 / (81.0 * cells)
    mf, mt = s[1] * one, s[2] * one
    vf = s[3] * two - mf * mf
    vt = s[4] * two - mt * mt
    cv = s[5] * two - mf * mt
    rmse = jnp.sqrt(s[0] * two)
    acc = cv / jnp.sqrt((vf + epsilon) * (vt + epsilon))
    for j in range(tiles):
        width_j = min(LANES, fields - j * LANES)
        span = pl.ds(j * LANES, width_j)
        rmse_ref[span] = rmse[j, :width_j]
        acc_ref[span] = acc[j, :width_j]
    small = [
        pltpu.make_async_copy(rmse_ref, rmse_hbm, sem.at[1]),
        pltpu.make_async_copy(acc_ref, acc_hbm, sem.at[2]),
    ]
    for other in small:
        other.start()
    for other in [copy, *small]:
        other.wait()


def local(nlat, nlon, predicted_state, observed_state, longterm_average_state):
    fields, rows, columns = predicted_state.shape
    tiles = pl.cdiv(fields, LANES)
    assert tiles == 2 and fields % 2 == 0
    flat = [
        x.reshape(fields * rows, columns)
        for x in (predicted_state, observed_state, longterm_average_state)
    ]
    edges = list(range(0, fields, CHUNK)) + [fields]
    bounds = tuple(zip(edges[:-1], edges[1:]))
    field_rows = pl.cdiv(fields, 16) * 16
    group = max(nlat, nlon)
    in_vmem = pltpu.VMEM((fields * rows, columns), jnp.bfloat16)
    blurred, totals = pl.pallas_call(
        functools.partial(kernel, nlat, nlon, fields, rows, bounds),
        out_shape=(
            jax.ShapeDtypeStruct((fields * rows, columns), jnp.bfloat16),
            jax.ShapeDtypeStruct((6 * tiles, LANES), F32),
        ),
        in_specs=[pl.BlockSpec(memory_space=pltpu.HBM)] * 3,
        out_specs=[pl.BlockSpec(memory_space=pltpu.VMEM)] * 2,
        scratch_shapes=[
            in_vmem, in_vmem, in_vmem,
            pltpu.VMEM((2, LANES * (rows + 1), LANES), F32),
            pltpu.VMEM((2, LANES * (rows + 1), LANES), F32),
            pltpu.VMEM((2, rows, LANES + 16, LANES), F32),
            pltpu.VMEM((2, rows, LANES + 16, LANES), F32),
            pltpu.VMEM((tiles, rows, LANES, LANES), F32),
            pltpu.VMEM((2, 2, tiles, LANES + 16, LANES), F32),
            pltpu.VMEM((2, 3, field_rows, LANES), F32),
            pltpu.VMEM((2, 3, field_rows, LANES), jnp.bfloat16),
            pltpu.VMEM((2, 3, field_rows, LANES), jnp.bfloat16),
            pltpu.VMEM((tiles, 2, rows, 2, LANES), F32),
            pltpu.VMEM((tiles, 2, rows + 2, 2, LANES), F32),
            pltpu.VMEM((2, 2, tiles, LANES, LANES), F32),
            pltpu.VMEM((rows, 8, LANES), F32),
            pltpu.VMEM((2, 6 * tiles, LANES), F32),
            pltpu.VMEM((2, group, 6 * tiles, LANES), F32),
            pltpu.SemaphoreType.DMA((len(bounds), 3)),
            pltpu.SemaphoreType.DMA((2,)),
            pltpu.SemaphoreType.DMA((2,)),
            pltpu.SemaphoreType.DMA((tiles, 2)),
            pltpu.SemaphoreType.DMA((tiles, 2)),
            pltpu.SemaphoreType.DMA((tiles, 4)),
            pltpu.SemaphoreType.DMA((tiles, 4)),
            pltpu.SemaphoreType.DMA((2, group)),
            pltpu.SemaphoreType.DMA((2, group)),
        ],
        compiler_params=pltpu.CompilerParams(
            collective_id=0, has_side_effects=True, vmem_limit_bytes=50 * 1024 * 1024
        ),
    )(*flat)
    blurred, rmse, acc = pl.pallas_call(
        functools.partial(finish, float(nlat * rows * nlon * columns), fields),
        out_shape=(
            jax.ShapeDtypeStruct((fields * rows, columns), jnp.bfloat16),
            jax.ShapeDtypeStruct((fields,), F32),
            jax.ShapeDtypeStruct((fields,), F32),
        ),
        in_specs=[pl.BlockSpec(memory_space=pltpu.VMEM)] * 2,
        out_specs=[pl.BlockSpec(memory_space=pltpu.HBM)] * 3,
        scratch_shapes=[
            pltpu.VMEM((fields,), F32),
            pltpu.VMEM((fields,), F32),
            pltpu.SemaphoreType.DMA((3,)),
        ],
        compiler_params=pltpu.CompilerParams(vmem_limit_bytes=8 * 1024 * 1024),
    )(blurred, totals)
    return (
        blurred.reshape(fields, rows, columns),
        rmse,
        acc,
    )


def solution(mesh):
    placed = (P(None, "lat", "lon"), P(None, "lat", "lon"), P(None, "lat", "lon"))
    return jax.shard_map(
        functools.partial(local, mesh.shape["lat"], mesh.shape["lon"]),
        mesh=mesh,
        in_specs=placed,
        out_specs=(P(None, "lat", "lon"), P(), P()),
        check_vma=False,
    )
```

time: 33.6 us -> 31.5 us (0.938)
  local copies, waits for them, and re-layouts: 2.5 us -> 0 us
  Pallas kernels: 30.4 us -> 30.8 us
    unnamed x3 -> x0, local copies, waits for them, and re-layouts: 2.5 us -> none
    pallas_call x0 -> x1, Pallas kernels: none -> 1.41 us  [local(): pl.pallas_call(functools.partial(finish, float(nlat * rows * nlon * colum...]
    pallas_call x1, Pallas kernels: 30.4 us -> 29.4 us  [local(): pl.pallas_call(functools.partial(kernel, nlat, nlon, fields, rows, bounds...]
where the time goes in v3:
time: 31.5 us; the launch traced here: 31.4 us
  Pallas kernels  30.8 us (98%)
  between operations  0.64 us (2%)
    pallas_call x1, Pallas kernels, local(): pl.pallas_call(functools.partial(kernel, nlat, nlon, fields, rows, bounds...  29.4 us
    pallas_call x1, Pallas kernels, local(): pl.pallas_call(functools.partial(finish, float(nlat * rows * nlon * colum...  1.41 us

profile of v3, /device:TPU:1, one launch (start us, length us, event | category | flops | bytes accessed | tf_op | source)
XLA Modules:
  0.0 31.4 jit_solution(8586464794122181815)
XLA Ops:
  0.6 29.4 %shard_map.58 = (bf16[8880,128]{1,0:T(8,128)(2,1)S(1)}, f32[12,128]{1,0:T(8,128)S(1)}) custom-call(bf16[8880,128]{1,0:T(8,128)(2,1)} %bitcast.4, bf16[8880,128]{1,0:T(8,128)(2,1)} %bitcast.5, bf16[8880,128]{1,0:T(8,128)(2,1)} %bitcast.6), custom_call_target="tpu_custom_call" | custom-call | tf_op jit(solution)/shard_map/pallas_call | solution.py:425
  30.0 1.4 %shard_map.59 = (bf16[8880,128]{1,0:T(8,128)(2,1)}, f32[222]{0:T(256)}, f32[222]{0:T(256)}) custom-call(bf16[8880,128]{1,0:T(8,128)(2,1)S(1)} %get-tuple-element.8.map_ref, f32[12,128]{1,0:T(8,128)S(1)} %get-tuple-element.9.tot_ref), custom_call_target="tpu_custom_call" | custom-call | tf_op jit(solution)/shard_map/pallas_call | solution.py:464

commit v4 on v3

--- a/solution.py
+++ b/solution.py
@@ -87,6 +87,8 @@
     for peer in greeted:
         pl.semaphore_signal(barrier, inc=1, device_id=peer, device_id_type=MESH)
 
+    nought = lon // nlon
+
     row = (lax.broadcasted_iota(jnp.int32, (rows, 8, LANES), 0) + lat * rows).astype(F32)
     cosine = jnp.cos(jnp.pi * (0.5 - row / (total_rows - 1)))
     weight[...] = cosine * (1.0 / mean_cosine(total_rows))
@@ -102,7 +104,7 @@
                 jnp.zeros(((rest + 7) // 8 * 8 * pitch, LANES), F32)
             )
     if edge.shape[2] > fields:
-        edge[:, :, fields:, :] = jnp.zeros((2, 3, edge.shape[2] - fields, LANES), F32)
+        edge[:, :, fields:, :] = jnp.zeros((2, 2, edge.shape[2] - fields, LANES), F32)
 
     def subtract(j, first, count):
         span = pl.ds(pl.multiple_of(first * rows, 16), count * rows)
@@ -112,11 +114,12 @@
             normal = three[2][q * rows : (q + 1) * rows]
             for a in range(2):
                 nat[j][a, into, :] = three[a][q * rows : (q + 1) * rows] - normal
-        for n in range(3):
-            for q in range(count):
-                for v, r in enumerate((0, rows - 1)):
-                    at = q * rows + r
-                    edge[v, n, pl.ds(first + q, 1), :] = three[n][at : at + 1, :]
+        for q in range(count):
+            for v, r in enumerate((0, rows - 1)):
+                at = q * rows + r
+                f, t, n = (x[at : at + 1, :] for x in three)
+                edge[v, 0, pl.ds(first + q, 1), :] = f - t
+                edge[v, 1, pl.ds(first + q, 1), :] = t - n
 
     def subtract_chunk(j, lo, hi):
         whole = (hi - lo) // STEP
@@ -159,7 +162,7 @@
             subtract_chunk(1, lo, hi)
 
     for v in range(2):
-        for n in range(3):
+        for n in range(2):
             edge_out[v, n] = edge[v, n].astype(jnp.bfloat16)
     pl.semaphore_wait(barrier, len(greeted))
     lat_copies = []
@@ -278,24 +281,33 @@
     lon_copies[1], cor_copies[1] = send_columns(1)
     accs[1] = lax.fori_loop(1, groups - 1, lambda g, acc: inner(1, g, acc), zero)
 
-    for j in range(tiles):
+    def side_groups(j, acc):
         for copy in lon_copies[j]:
             copy.wait_recv()
         take_columns(j)
-        accs[j] = lax.fori_loop(
-            0, 2, lambda g, acc, j=j: inner(j, g * (groups - 1), acc), accs[j]
+        return lax.fori_loop(
+            0, 2, lambda g, acc: inner(j, g * (groups - 1), acc), acc
         )
 
+    accs[0] = side_groups(0, accs[0])
     for copy in lat_copies:
         copy.wait_recv()
     tail = edge_in.shape[2] - LANES
     for v in range(2):
-        normal = edge_in[v, 2].astype(F32)
-        for a in range(2):
-            t = edge_in[v, a].astype(F32) - normal
+        true = edge_in[v, 1].astype(F32)
+        for a, t in enumerate((edge_in[v, 0].astype(F32) + true, true)):
             t = jnp.concatenate([t, jnp.zeros((LANES - tail, LANES), F32)], axis=0)
             for j in range(tiles):
                 halo[v, a, j, pl.ds(8, LANES), :] = t[j * LANES : (j + 1) * LANES, :].T
+    for j in range(tiles):
+
+        def outer_seven(i, acc, j=j):
+            for q in range(7):
+                acc = outer(j, i * 7 + q + 1, acc)
+            return acc
+
+        accs[j] = lax.fori_loop(0, (groups - 2) // 7, outer_seven, accs[j])
+    accs[1] = side_groups(1, accs[1])
     for j in range(tiles):
         for copy in cor_copies[j]:
             copy.wait_recv()
@@ -303,13 +315,8 @@
             for v, r in enumerate((0, rows + 1)):
                 for a in range(2):
                     halo[v, a, j, pl.ds(column, 1), :] = side_in[j, s, r, pl.ds(a, 1), :]
-
-        def outer_four(i, acc, j=j):
-            for q in range(4):
-                acc = outer(j, i * 4 + q, acc)
-            return acc
-
-        accs[j] = lax.fori_loop(0, groups // 4, outer_four, accs[j])
+        for g in (0, groups - 1):
+            accs[j] = outer(j, g + nought, accs[j])
 
     for j in range(tiles):
         for n in range(6):
@@ -372,13 +379,12 @@
             return carry
 
         lax.fori_loop(0, count // 2, narrow, 0)
-    arrive1()
-    tot_ref[...] = added(1, len(line_peers) + 1)
-
     for copy in lat_copies + sum(lon_copies + cor_copies, []):
         copy.wait_send()
     drain0()
     drain1()
+    arrive1()
+    tot_ref[...] = added(1, len(line_peers) + 1)
 
 
 def finish(cells, fields, map_ref, tot_ref, out_hbm, rmse_hbm, acc_hbm, rmse_ref, acc_ref, sem):
@@ -438,9 +444,9 @@
             pltpu.VMEM((2, rows, LANES + 16, LANES), F32),
             pltpu.VMEM((tiles, rows, LANES, LANES), F32),
             pltpu.VMEM((2, 2, tiles, LANES + 16, LANES), F32),
-            pltpu.VMEM((2, 3, field_rows, LANES), F32),
-            pltpu.VMEM((2, 3, field_rows, LANES), jnp.bfloat16),
-            pltpu.VMEM((2, 3, field_rows, LANES), jnp.bfloat16),
+            pltpu.VMEM((2, 2, field_rows, LANES), F32),
+            pltpu.VMEM((2, 2, field_rows, LANES), jnp.bfloat16),
+            pltpu.VMEM((2, 2, field_rows, LANES), jnp.bfloat16),
             pltpu.VMEM((tiles, 2, rows, 2, LANES), F32),
             pltpu.VMEM((tiles, 2, rows + 2, 2, LANES), F32),
             pltpu.VMEM((2, 2, tiles, LANES, LANES), F32),

time: 31.5 us -> 30.1 us (0.956)
  Pallas kernels: 30.8 us -> 29.3 us
    pallas_call x1, Pallas kernels: 29.4 us -> 27.9 us  [local(): pl.pallas_call(functools.partial(kernel, nlat, nlon, fields, rows, bounds...]
where the time goes in v4:
time: 30.1 us; the launch traced here: 30 us
  Pallas kernels  29.3 us (97%)
  between operations  0.64 us (2%)
    pallas_call x1, Pallas kernels, local(): pl.pallas_call(functools.partial(kernel, nlat, nlon, fields, rows, bounds...  27.9 us
    pallas_call x1, Pallas kernels, local(): pl.pallas_call(functools.partial(finish, float(nlat * rows * nlon * colum...  1.41 us

profile of v4, /device:TPU:1, one launch (start us, length us, event | category | flops | bytes accessed | tf_op | source)
XLA Modules:
  0.0 30.0 jit_solution(9123012442632087414)
XLA Ops:
  0.6 27.9 %shard_map.58 = (bf16[8880,128]{1,0:T(8,128)(2,1)S(1)}, f32[12,128]{1,0:T(8,128)S(1)}) custom-call(bf16[8880,128]{1,0:T(8,128)(2,1)} %bitcast.4, bf16[8880,128]{1,0:T(8,128)(2,1)} %bitcast.5, bf16[8880,128]{1,0:T(8,128)(2,1)} %bitcast.6), custom_call_target="tpu_custom_call" | custom-call | tf_op jit(solution)/shard_map/pallas_call | solution.py:431
  28.6 1.4 %shard_map.59 = (bf16[8880,128]{1,0:T(8,128)(2,1)}, f32[222]{0:T(256)}, f32[222]{0:T(256)}) custom-call(bf16[8880,128]{1,0:T(8,128)(2,1)S(1)} %get-tuple-element.8.map_ref, f32[12,128]{1,0:T(8,128)S(1)} %get-tuple-element.9.tot_ref), custom_call_target="tpu_custom_call" | custom-call | tf_op jit(solution)/shard_map/pallas_call | solution.py:470

commit v5 on v4

--- a/solution.py
+++ b/solution.py
@@ -14,7 +14,7 @@
 LANES = 128
 STEP = 8
 AT_ONCE = 7
-CHUNK = 64
+CHUNK = 32
 
 
 def mean_cosine(rows):
@@ -353,7 +353,7 @@
             x = x + got[stage, k]
         return x
 
-    arrive0, drain0 = exchange(0, x * 4 + y, plane_peers)
+    arrive0, drain0 = exchange(0, z * 2 + core, line_peers)
 
     def turn_back(r, carry):
         for j in range(tiles):
@@ -363,8 +363,8 @@
 
     lax.fori_loop(0, rows // 2, turn_back, 0)
     arrive0()
-    sums[1] = added(0, len(plane_peers) + 1)
-    arrive1, drain1 = exchange(1, z * 2 + core, line_peers)
+    sums[1] = added(0, len(line_peers) + 1)
+    arrive1, drain1 = exchange(1, x * 4 + y, plane_peers)
     lax.fori_loop(rows // 2, rows, turn_back, 0)
 
     for j in range(tiles):
@@ -384,7 +384,7 @@
     drain0()
     drain1()
     arrive1()
-    tot_ref[...] = added(1, len(line_peers) + 1)
+    tot_ref[...] = added(1, len(plane_peers) + 1)
 
 
 def finish(cells, fields, map_ref, tot_ref, out_hbm, rmse_hbm, acc_hbm, rmse_ref, acc_ref, sem):

time: 30.1 us -> 29.8 us (0.990)
  no operation moved by 1% of the time
where the time goes in v5:
time: 29.8 us; the launch traced here: 29.7 us
  Pallas kernels  29.1 us (98%)
  between operations  0.64 us (2%)
    pallas_call x1, Pallas kernels, local(): pl.pallas_call(functools.partial(kernel, nlat, nlon, fields, rows, bounds...  27.7 us
    pallas_call x1, Pallas kernels, local(): pl.pallas_call(functools.partial(finish, float(nlat * rows * nlon * colum...  1.41 us

profile of v5, /device:TPU:1, one launch (start us, length us, event | category | flops | bytes accessed | tf_op | source)
XLA Modules:
  0.0 29.7 jit_solution(6245428357177628539)
XLA Ops:
  0.6 27.7 %shard_map.58 = (bf16[8880,128]{1,0:T(8,128)(2,1)S(1)}, f32[12,128]{1,0:T(8,128)S(1)}) custom-call(bf16[8880,128]{1,0:T(8,128)(2,1)} %bitcast.4, bf16[8880,128]{1,0:T(8,128)(2,1)} %bitcast.5, bf16[8880,128]{1,0:T(8,128)(2,1)} %bitcast.6), custom_call_target="tpu_custom_call" | custom-call | tf_op jit(solution)/shard_map/pallas_call | solution.py:431
  28.3 1.4 %shard_map.59 = (bf16[8880,128]{1,0:T(8,128)(2,1)}, f32[222]{0:T(256)}, f32[222]{0:T(256)}) custom-call(bf16[8880,128]{1,0:T(8,128)(2,1)S(1)} %get-tuple-element.8.map_ref, f32[12,128]{1,0:T(8,128)S(1)} %get-tuple-element.9.tot_ref), custom_call_target="tpu_custom_call" | custom-call | tf_op jit(solution)/shard_map/pallas_call | solution.py:470
